TPU v7x, 128 devices: a whole 4x4x4 slice. The times are simulated.
128 devices in a mesh: rep: 2 (over core), dp: 64 (over x, y, z).
Axes of the slice: x: 4, y: 4, z: 4, core: 2. Of those that a mesh axis runs over, the one named last changes fastest.
Arguments:
- x: bfloat16 [128, 2048, 512], P(('rep', 'dp')), parts along dimension 0
- dy: bfloat16 [128, 2048, 512], P(('rep', 'dp')), parts along dimension 0
- w_gate: bfloat16 [2, 512, 4096], replicated
- w_up: bfloat16 [2, 512, 4096], replicated
- w_down: bfloat16 [2, 4096, 512], replicated
- m_w_gate: float32 [2, 512, 4096], replicated
- m_w_up: float32 [2, 512, 4096], replicated
- m_w_down: float32 [2, 4096, 512], replicated
- v_w_gate: float32 [2, 512, 4096], replicated
- v_w_up: float32 [2, 512, 4096], replicated
- v_w_down: float32 [2, 4096, 512], replicated
Outputs:
- output 1: bfloat16 [4, 512, 4096], P('rep'), parts along dimension 0
- output 2: bfloat16 [4, 512, 4096], P('rep'), parts along dimension 0
- output 3: bfloat16 [4, 4096, 512], P('rep'), parts along dimension 0
- output 4: float32 [4, 512, 4096], P('rep'), parts along dimension 0
- output 5: float32 [4, 512, 4096], P('rep'), parts along dimension 0
- output 6: float32 [4, 4096, 512], P('rep'), parts along dimension 0
- output 7: float32 [4, 512, 4096], P('rep'), parts along dimension 0
- output 8: float32 [4, 512, 4096], P('rep'), parts along dimension 0
- output 9: float32 [4, 4096, 512], P('rep'), parts along dimension 0
There are 2 independent parts. A program takes and returns all parts, laid end to end along the dimension named above; an argument that names none is the same for every part.
All inputs are finite; a program needn't handle non-finite values.
Results may differ from a plain program's by a relative error of at most 0.022.
Values are sent between devices in bfloat16 or wider.
A program may use at most 1.5 GiB of HBM per device.

v0:
```python
import jax
import jax.numpy as jnp
from jax import lax
from jax.sharding import PartitionSpec as P

NAMES = ("w_gate", "w_up", "w_down")


def matmul(a, w):
    return jnp.dot(a, w, preferred_element_type=jnp.float32).astype(jnp.bfloat16)


def normed(h):
    wide = h.astype(jnp.float32)
    scale = lax.rsqrt(jnp.mean(wide**2, -1, keepdims=True) + 1e-6)
    return (wide * scale).astype(jnp.bfloat16)


def layer(h, w):
    a = normed(h)
    gate = jnp.dot(a, w["w_gate"], preferred_element_type=jnp.float32)
    up = jnp.dot(a, w["w_up"], preferred_element_type=jnp.float32)
    return h + matmul((jax.nn.silu(gate) * up).astype(jnp.bfloat16), w["w_down"])


def adamw(w, m, v, g):
    m = 0.9 * m + 0.1 * g
    v = 0.95 * v + 0.05 * g * g
    step = m * lax.rsqrt(v + 1e-8) + 0.1 * w
    return (w - 0.02 * step).astype(jnp.bfloat16), m, v


def clipped(gradients, sum_of_squares, count):
    factor = jnp.minimum(1.0, 0.5 * lax.rsqrt(sum_of_squares / count + 1e-30))
    return [g * factor for g in gradients]


def solution(mesh):
    def step(x, dy, *arrays):
        weights, m, v = (arrays[i : i + 3] for i in (0, 3, 6))
        layers = weights[0].shape[0]
        h, kept = x[0], []
        for number in range(layers):
            kept.append(h)
            h = layer(h, {name: w[number] for name, w in zip(NAMES, weights, strict=True)})
        by_h, summed = dy[0], [None] * layers
        for number in reversed(range(layers)):
            _, back = jax.vjp(lambda w, h: layer(h, w), {name: w[number] for name, w in zip(NAMES, weights, strict=True)}, kept[number])
            by_w, by_h = back(by_h)
            summed[number] = [lax.psum(by_w[name], "dp") for name in NAMES]
        gradients = [jnp.stack([summed[number][i] for number in range(layers)]).astype(jnp.float32) for i in range(3)]
        gradients = clipped(gradients, sum(jnp.sum(g * g) for g in gradients), sum(g.size for g in gradients))
        new = [adamw(w.astype(jnp.float32), m, v, g) for w, m, v, g in zip(weights, m, v, gradients, strict=True)]
        return tuple(one[which] for which in range(3) for one in new)

    return jax.shard_map(
        step,
        mesh=mesh,
        in_specs=(P(("rep", "dp"), None, None),) * 2 + (P(None, None, None),) * 9,
        out_specs=(P("rep", None, None),) * 9,
        check_vma=False,
    )
```

profile of v0, /device:TPU:0, one launch (start us, length us, event | category | flops | bytes accessed | tf_op | source)
XLA Modules:
  0.0 724.7 jit_solution(15568569532999853013)
XLA Ops:
  7.2 0.0 all-reduce.3.cloned.1.call-start
  7.2 2.9 copy.20
  10.2 0.0 copy-start.4
  10.2 0.5 fusion.51
  10.6 4.2 copy.21
  14.8 15.2 %convolution_convert_fusion.1 = bf16[2048,4096]{1,0:T(8,128)(2,1)} fusion(bf16[2,4096,512]{2,1,0:T(8,128)(2,1)} %param.15, bf16[1,2048,512]{2,1,0:T(8,128)(2,1)} %param.12), kind=kOutput, calls=%fused_computation.61 | convolution fusion | flops 8598323200 | bytes 23068672 | tf_op jit(solution)/shard_map/transpose(jvp())/dot_general | solution.py:10
  30.0 0.0 copy-done.7
  30.0 16.9 %fusion.71 = f32[2048,4096]{1,0:T(8,128)} fusion(bf16[2,512,4096]{2,1,0:T(8,128)(2,1)} %param.13, bf16[1,2048,512]{2,1,0:T(8,128)(2,1)S(1)} %copy-done.7, f32[2048]{0:T(1024)S(1)} %add_rsqrt_fusion), kind=kOutput, calls=%fused_computation.104 | convolution fusion | flops 8593080320 | bytes 39854080 | tf_op jit(solution)/shard_map/dot_general | solution.py:21
  46.9 0.0 copy-done.15
  46.9 32.7 %multiply_convert_fusion.1 = (bf16[2048,4096]{1,0:T(8,128)(2,1)}, f32[2048,4096]{1,0:T(8,128)}) fusion(f32[2048,4096]{1,0:T(8,128)} %fusion.71, bf16[2,512,4096]{2,1,0:T(8,128)(2,1)} %param.14, bf16[1,2048,512]{2,1,0:T(8,128)(2,1)} %param.11, f32[2048]{0:T(1024)S(1)} %add_rsqrt_fusion), kind=kOutput, calls=%fused_computation.17 | convolution fusion | flops 8643411968 | bytes 90185728 | tf_op jit(solution)/shard_map/dot_general | solution.py:22
  79.6 0.0 copy-done.4
  79.6 15.0 %fusion.55 = (f32[2048]{0:T(1024)S(1)}, bf16[2048,512]{0,1:T(8,128)(2,1)}) fusion(bf16[2048,4096]{1,0:T(8,128)(2,1)} %get-tuple-element.24, bf16[2,4096,512]{2,1,0:T(8,128)(2,1)} %param.15, bf16[1,2048,512]{1,2,0:T(8,128)(2,1)S(1)} %copy.20), kind=kOutput, calls=%fused_computation.88 | convolution fusion | flops 8595175424 | bytes 25174016 | tf_op jit(solution)/shard_map/dot_general | solution.py:10
  94.7 0.0 copy-start.13
  94.7 0.0 copy-start.9
  94.7 18.0 %fusion.58 = f32[2048,4096]{1,0:T(8,128)} fusion(bf16[2,512,4096]{2,1,0:T(8,128)(2,1)} %param.14, bf16[2048,512]{0,1:T(8,128)(2,1)} %get-tuple-element.27, f32[2048]{0:T(1024)S(1)} %fusion.109), kind=kOutput, calls=%fused_computation.91 | convolution fusion | flops 8593080320 | bytes 39854080 | tf_op jit(solution)/shard_map/jvp()/dot_general | solution.py:22
  112.6 0.0 copy-done.11
  112.6 0.0 copy-done.13
  112.7 0.0 copy-done.9
  112.7 39.7 %fusion.2 = (bf16[2048,4096]{1,0:T(8,128)(2,1)}, f32[2048,4096]{1,0:T(8,128)}) fusion(f32[2048,4096]{1,0:T(8,128)} %fusion.58, bf16[2048,4096]{1,0:T(8,128)(2,1)} %convolution_convert_fusion.1, bf16[2,512,4096]{2,1,0:T(8,128)(2,1)} %param.13, bf16[2048,512]{0,1:T(8,128)(2,1)S(1)} %copy-done.9, f32[2048]{0:T(1024)S(1)} %fusion.109), kind=kOutput, calls=%fused_computation.8 | convolution fusion | flops 8693743616 | bytes 106962944 | tf_op jit(solution)/shard_map/jvp()/dot_general | solution.py:21
  152.3 20.7 %fusion.88 = bf16[2048,512]{0,1:T(8,128)(2,1)} fusion(bf16[2,512,4096]{2,1,0:T(8,128)(2,1)} %param.14, bf16[2048,4096]{1,0:T(8,128)(2,1)} %convolution_convert_fusion.1, f32[2048,4096]{1,0:T(8,128)} %get-tuple-element.29), kind=kOutput, calls=%fused_computation.118 | convolution fusion | flops 8641314816 | bytes 56623104 | tf_op jit(solution)/shard_map/transpose(jvp())/dot_general | solution.py:22
  173.0 0.0 copy-done.8
  173.0 26.1 %fusion.44 = bf16[1,4096,512]{2,1,0:T(8,128)(2,1)} fusion(f32[2048,4096]{1,0:T(8,128)} %fusion.58, bf16[1,2048,512]{2,1,0:T(8,128)(2,1)S(1)} %copy-done.8, f32[2048,4096]{1,0:T(8,128)} %get-tuple-element.29), kind=kOutput, calls=%fused_computation.76 | convolution fusion | flops 8642363392 | bytes 73400320 | tf_op jit(solution)/shard_map/transpose(jvp())/dot_general | solution.py:10
  199.0 0.0 copy-start.14
  199.1 15.2 %fusion.57 = (f32[2048]{0:T(1024)S(1)}, bf16[2048,512]{0,1:T(8,128)(2,1)S(1)}) fusion(bf16[2048,512]{0,1:T(8,128)(2,1)} %get-tuple-element.27, bf16[2048,512]{0,1:T(8,128)(2,1)} %fusion.88, bf16[2048,4096]{1,0:T(8,128)(2,1)} %get-tuple-element.28, bf16[2,512,4096]{2,1,0:T(8,128)(2,1)} %param.13), kind=kOutput, calls=%fused_computation.90 | convolution fusion | flops 8595175424 | bytes 27271168 | tf_op jit(solution)/shard_map/transpose(jvp())/dot_general | solution.py:21
  214.2 0.0 copy-done.12
  214.3 0.0 copy-done.6
  214.3 0.0 copy-done.10
  214.3 0.0 copy-done.14
  214.3 1.4 fusion.98
  215.7 14.0 %fusion.45 = bf16[1,4096,512]{2,1,0:T(8,128)(2,1)} fusion(bf16[2048,4096]{1,0:T(8,128)(2,1)} %get-tuple-element.24, bf16[2048,512]{0,1:T(8,128)(2,1)S(1)} %fusion.98), kind=kOutput, calls=%fused_computation.77 | convolution fusion | flops 8592031744 | bytes 23068672 | tf_op jit(solution)/shard_map/transpose(jvp())/dot_general | solution.py:10
  229.7 15.0 %convolution_convert_fusion = bf16[2048,4096]{1,0:T(8,128)(2,1)} fusion(bf16[2048,512]{0,1:T(8,128)(2,1)S(1)} %fusion.98, bf16[2,4096,512]{2,1,0:T(8,128)(2,1)} %param.15), kind=kOutput, calls=%fused_computation.60 | convolution fusion | flops 8598323200 | bytes 23068672 | tf_op jit(solution)/shard_map/transpose(jvp())/dot_general | solution.py:10
  244.6 21.6 %fusion.46 = bf16[1,512,4096]{2,1,0:T(8,128)(2,1)} fusion(bf16[2048,4096]{1,0:T(8,128)(2,1)} %convolution_convert_fusion.1, bf16[2048,512]{0,1:T(8,128)(2,1)S(1)} %copy-done.10, f32[2048]{0:T(1024)S(1)} %copy-done.14, f32[2048,4096]{1,0:T(8,128)} %get-tuple-element.29), kind=kOutput, calls=%fused_computation.78 | convolution fusion | flops 8645509120 | bytes 56631296 | tf_op jit(solution)/shard_map/transpose(jvp())/dot_general | solution.py:22
  266.2 13.9 %fusion.43 = bf16[1,512,4096]{2,1,0:T(8,128)(2,1)} fusion(bf16[2048,4096]{1,0:T(8,128)(2,1)} %get-tuple-element.28, bf16[2048,512]{0,1:T(8,128)(2,1)S(1)} %copy-done.10, f32[2048]{0:T(1024)S(1)} %copy-done.14), kind=kOutput, calls=%fused_computation.75 | convolution fusion | flops 8593080320 | bytes 23076864 | tf_op jit(solution)/shard_map/transpose(jvp())/dot_general | solution.py:21
  280.1 0.0 copy-done.5
  280.1 0.0 copy-done.16
  280.1 22.0 %fusion.47 = bf16[1,512,4096]{2,1,0:T(8,128)(2,1)} fusion(bf16[2048,4096]{1,0:T(8,128)(2,1)} %convolution_convert_fusion, f32[2048,4096]{1,0:T(8,128)} %fusion.71, bf16[1,2048,512]{1,2,0:T(8,128)(2,1)S(1)} %copy-done.5, f32[2048]{0:T(1024)S(1)} %copy-done.16), kind=kOutput, calls=%fused_computation.79 | convolution fusion | flops 8645509120 | bytes 56631296 | tf_op jit(solution)/shard_map/transpose(jvp())/dot_general | solution.py:22
  302.1 32.2 %fusion.48 = bf16[1,512,4096]{2,1,0:T(8,128)(2,1)} fusion(f32[2048,4096]{1,0:T(8,128)} %fusion.71, f32[2048,4096]{1,0:T(8,128)} %get-tuple-element.25, bf16[2048,4096]{1,0:T(8,128)(2,1)} %convolution_convert_fusion, bf16[1,2048,512]{1,2,0:T(8,128)(2,1)S(1)} %copy-done.5, f32[2048]{0:T(1024)S(1)} %copy-done.16), kind=kOutput, calls=%fused_computation.80 | convolution fusion | flops 8687452160 | bytes 90185728 | tf_op jit(solution)/shard_map/transpose(jvp())/dot_general | solution.py:21
  334.3 0.0 all-reduce.3.cloned.1.call-update
  334.3 274.9 %all-reduce.3.cloned.1.call-done = (bf16[1,512,4096]{2,1,0:T(8,128)(2,1)}, bf16[1,512,4096]{2,1,0:T(8,128)(2,1)}, bf16[1,512,4096]{2,1,0:T(8,128)(2,1)}, bf16[1,...) async-done(((bf16[1,512,4096]{2,1,0:T(8,128)(2,1)}, bf16[1,512,4096]{2,1,0:T(8,128)(2,1)}, bf16[1,512,4096]{2,1,0:T(8,128)(2,1)}, ...) | async-done | bytes 25165840 | tf_op jit(solution)/shard_map/psum | solution.py:50
  609.2 7.8 %fusion.24 = f32[]{:T(128)} fusion(bf16[1,4096,512]{2,1,0:T(8,128)(2,1)} %get-tuple-element.13, bf16[1,4096,512]{2,1,0:T(8,128)(2,1)} %get-tuple-element.14), kind=kLoop, calls=%fused_computation.48 | loop fusion | flops 16777215 | bytes 8388612 | tf_op jit(solution)/shard_map/reduce_sum | solution.py:52
  617.0 7.0 fusion.23
  624.1 0.0 copy-done
  624.1 0.0 copy-done.2
  624.1 4.9 fusion.22
  631.0 0.0 copy-start.1
  631.0 30.6 %fusion.30 = (bf16[2,4096,512]{2,1,0:T(8,128)(2,1)}, f32[2,4096,512]{2,1,0:T(8,128)}, f32[2,4096,512]{2,1,0:T(8,128)}) fusion(bf16[2,4096,512]{2,1,0:T(8,128)(2,1)} %param.15, f32[]{:T(128)S(6)} %min_shard_map.3, bf16[1,4096,512]{2,1,0:T(8,128)(2,1)} %get-tuple-element.13, bf16[1,4096,512]{2,1,0:T(8,128)(2,1)} %get-tuple-element.14, ...), kind=kLoop, calls=%fused_computation.54 | loop fusion | flops 83886080 | bytes 92274688 | tf_op jit(solution)/shard_map/convert_element_type | solution.py:30
  661.7 0.0 copy-done.1
  661.7 56.0 %fusion.21 = (bf16[2,512,4096]{2,1,0:T(8,128)(2,1)}, f32[2,512,4096]{2,1,0:T(8,128)}, f32[2,512,4096]{2,1,0:T(8,128)}, bf16[2,512,4096]{2,1,0:T(8,128)(2,1)}, f3...) fusion(bf16[2,512,4096]{2,1,0:T(8,128)(2,1)} %param.13, f32[]{:T(128)S(6)} %min_shard_map.3, ...), kind=kLoop, calls=%fused_computation.45 | loop fusion | flops 167772160 | bytes 184549376 | tf_op jit(solution)/shard_map/convert_element_type | solution.py:30
  (16 shorter events, 0.1 us)
Async XLA Ops:
  7.2 602.0 %all-reduce.3.cloned.1.call-start = ((), (), s32[]{:S(2)}) async-start(), calls=%async_computation | async-start | bytes 50331648 | tf_op jit(solution)/shard_map/psum | solution.py:50
  10.2 69.5 %copy-start.4 = (bf16[1,2048,512]{1,2,0:T(8,128)(2,1)}, bf16[1,2048,512]{1,2,0:T(8,128)(2,1)S(1)}, u32[]{:S(2)}) copy-start(bf16[1,2048,512]{1,2,0:T(8,128)(2,1)S(1)} %copy.20) | copy-start | bytes 6291460
  10.6 36.3 %copy-start.15 = (f32[2048]{0:T(1024)}, f32[2048]{0:T(1024)S(1)}, u32[]{:S(2)}) copy-start(f32[2048]{0:T(1024)S(1)} %add_rsqrt_fusion) | copy-start | bytes 24580
  14.8 15.2 %copy-start.7 = (bf16[1,2048,512]{2,1,0:T(8,128)(2,1)S(1)}, bf16[1,2048,512]{2,1,0:T(8,128)(2,1)}, u32[]{:S(2)}) copy-start(bf16[1,2048,512]{2,1,0:T(8,128)(2,1)} %param.11) | copy-start | bytes 6291460
  94.7 18.0 %copy-start.11 = (f32[2048]{0:T(1024)}, f32[2048]{0:T(1024)S(1)}, u32[]{:S(2)}) copy-start(f32[2048]{0:T(1024)S(1)} %get-tuple-element.26) | copy-start | bytes 24580
  94.7 18.0 %copy-start.13 = (f32[2048]{0:T(1024)}, f32[2048]{0:T(1024)S(1)}, u32[]{:S(2)}) copy-start(f32[2048]{0:T(1024)S(1)} %fusion.109) | copy-start | bytes 24580
  94.7 18.0 %copy-start.9 = (bf16[2048,512]{0,1:T(8,128)(2,1)S(1)}, bf16[2048,512]{0,1:T(8,128)(2,1)}, u32[]{:S(2)}) copy-start(bf16[2048,512]{0,1:T(8,128)(2,1)} %get-tuple-element.27) | copy-start | bytes 6291460
  152.3 20.7 %copy-start.8 = (bf16[1,2048,512]{2,1,0:T(8,128)(2,1)S(1)}, bf16[1,2048,512]{2,1,0:T(8,128)(2,1)}, u32[]{:S(2)}) copy-start(bf16[1,2048,512]{2,1,0:T(8,128)(2,1)} %param.12) | copy-start | bytes 6291460
  199.0 15.2 %copy-start.12 = (f32[2048]{0:T(1024)S(1)}, f32[2048]{0:T(1024)}, u32[]{:S(2)}) copy-start(f32[2048]{0:T(1024)} %copy-done.11) | copy-start | bytes 24580
  199.0 15.2 %copy-start.6 = (bf16[1,2048,512]{1,2,0:T(8,128)(2,1)S(1)}, bf16[1,2048,512]{1,2,0:T(8,128)(2,1)}, u32[]{:S(2)}) copy-start(bf16[1,2048,512]{1,2,0:T(8,128)(2,1)} %copy.21) | copy-start | bytes 6291460
  199.0 15.2 %copy-start.10 = (bf16[2048,512]{0,1:T(8,128)(2,1)S(1)}, bf16[2048,512]{0,1:T(8,128)(2,1)}, u32[]{:S(2)}) copy-start(bf16[2048,512]{0,1:T(8,128)(2,1)} %get-tuple-element.27) | copy-start | bytes 6291460
  199.0 15.2 %copy-start.14 = (f32[2048]{0:T(1024)S(1)}, f32[2048]{0:T(1024)}, u32[]{:S(2)}) copy-start(f32[2048]{0:T(1024)} %copy-done.13) | copy-start | bytes 24580
  266.2 13.9 %copy-start.5 = (bf16[1,2048,512]{1,2,0:T(8,128)(2,1)S(1)}, bf16[1,2048,512]{1,2,0:T(8,128)(2,1)}, u32[]{:S(2)}) copy-start(bf16[1,2048,512]{1,2,0:T(8,128)(2,1)} %copy-done.4) | copy-start | bytes 6291460
  266.2 13.9 %copy-start.16 = (f32[2048]{0:T(1024)S(1)}, f32[2048]{0:T(1024)}, u32[]{:S(2)}) copy-start(f32[2048]{0:T(1024)} %copy-done.15) | copy-start | bytes 24580
  609.2 14.9 %copy-start = (bf16[1,512,4096]{2,1,0:T(8,128)(2,1)S(1)}, bf16[1,512,4096]{2,1,0:T(8,128)(2,1)}, u32[]{:S(2)}) copy-start(bf16[1,512,4096]{2,1,0:T(8,128)(2,1)} %get-tuple-element.9) | copy-start | bytes 12582916
  609.2 14.9 %copy-start.2 = (bf16[1,512,4096]{2,1,0:T(8,128)(2,1)S(1)}, bf16[1,512,4096]{2,1,0:T(8,128)(2,1)}, u32[]{:S(2)}) copy-start(bf16[1,512,4096]{2,1,0:T(8,128)(2,1)} %get-tuple-element.10) | copy-start | bytes 12582916
  631.0 30.7 %copy-start.1 = (bf16[1,512,4096]{2,1,0:T(8,128)(2,1)S(1)}, bf16[1,512,4096]{2,1,0:T(8,128)(2,1)}, u32[]{:S(2)}) copy-start(bf16[1,512,4096]{2,1,0:T(8,128)(2,1)} %get-tuple-element.9) | copy-start | bytes 12582916
  631.0 30.7 %copy-start.3 = (bf16[1,512,4096]{2,1,0:T(8,128)(2,1)S(1)}, bf16[1,512,4096]{2,1,0:T(8,128)(2,1)}, u32[]{:S(2)}) copy-start(bf16[1,512,4096]{2,1,0:T(8,128)(2,1)} %get-tuple-element.10) | copy-start | bytes 12582916
Sparse Core Ops, SparseCore 0:
  334.4 274.7 all-reduce.2
where the time goes:
time: 732 us; the launch traced here: 725 us
  matrix products  318 us (43%)
  waiting for transfers between devices  275 us (38%)
  other arithmetic  108 us (15%)
  between operations  16.4 us (2%)
    psum x1, waiting for transfers between devices, step(): summed[number] = [lax.psum(by_w[name], 'dp') for name in NAMES]  275 us
    dot_general x5, matrix products, layer(): gate = jnp.dot(a, w['w_gate'], preferred_element_type=jnp.float32)  118 us
    dot_general x5, matrix products, layer(): up = jnp.dot(a, w['w_up'], preferred_element_type=jnp.float32)  115 us
    convert_element_type x2, other arithmetic, adamw(): return ((w - 0.02 * step).astype(jnp.bfloat16), m, v)  86.6 us
    dot_general x5, matrix products, matmul(): jnp.dot(a, w, preferred_element_type=jnp.float32).astype(jnp.bfloat16)  85.2 us
    reduce_sum x3, other arithmetic, step(): jnp.sum(g * g)  19.8 us
  transfers between devices with their start and end apart: 1, of which 1 were waited for; matrix products, arithmetic and copies ran while one was open for 0% of the time, Pallas kernels for 0%

commit v1 on v0

v1 whole, which is shorter than its diff:
```python
import functools

import jax
import jax.numpy as jnp
from jax import lax
from jax.experimental import pallas as pl
from jax.experimental.pallas import tpu as pltpu
from jax.sharding import PartitionSpec as P

NAMES = ("w_gate", "w_up", "w_down")
T, D, FF, LAYERS = 2048, 512, 4096, 2
CH = 512
PER = FF // CH
N = PER * LAYERS
TILE = 512
PHASES = T // TILE
COLOURS = 6
ROWS = 1024
AT = [3 + o for o in (0, 2, 4, 5, 6, 7, 8, 9, 10, 11, 12, 14, 16, 17)]
ACCS, GATHERS = 3, 4
VMEM_LIMIT = 66_000_000

dot = functools.partial(lax.dot_general, preferred_element_type=jnp.float32)
NN = (((1,), (0,)), ((), ()))
NT = (((1,), (1,)), ((), ()))
TN = (((0,), (0,)), ((), ()))


def scale_of(wide):
    return lax.rsqrt(jnp.mean(wide * wide, -1, keepdims=True) + 1e-6)


def normed(h):
    wide = h.astype(jnp.float32)
    return (wide * scale_of(wide)).astype(jnp.bfloat16)


def forward_kernel(x_ref, wg_ref, wu_ref, wd_ref, h_ref, a_ref):
    x = x_ref[...]
    a = normed(x)
    a_ref[1] = a
    y = jnp.zeros(x.shape, jnp.float32)
    for c in range(FF // CH):
        at = pl.ds(c * CH, CH)
        gate = dot(a, wg_ref[0, :, at], NN)
        up = dot(a, wu_ref[0, :, at], NN)
        p = (gate * (1 / (1 + jnp.exp(-gate))) * up).astype(jnp.bfloat16)
        y += dot(p, wd_ref[0, at, :], NN)
    h = (x.astype(jnp.float32) + y.astype(jnp.bfloat16).astype(jnp.float32)).astype(jnp.bfloat16)
    h_ref[...] = h
    a_ref[0] = normed(h)


def forward(x, wg, wu, wd):
    tile = 256
    whole = lambda s: pl.BlockSpec(s, lambda i: (0, 0, 0), pipeline_mode=pl.Buffered(1))
    return pl.pallas_call(
        forward_kernel,
        grid=(T // tile,),
        in_specs=[pl.BlockSpec((tile, D), lambda i: (i, 0)), whole((1, D, FF)), whole((1, D, FF)), whole((1, FF, D))],
        out_specs=[pl.BlockSpec((tile, D), lambda i: (i, 0)), pl.BlockSpec((2, tile, D), lambda i: (0, i, 0))],
        out_shape=[jax.ShapeDtypeStruct((T, D), jnp.bfloat16), jax.ShapeDtypeStruct((2, T, D), jnp.bfloat16)],
        compiler_params=pltpu.CompilerParams(vmem_limit_bytes=VMEM_LIMIT),
    )(x, wg, wu, wd)


def place(stage):
    return ROWS - (ROWS >> stage)


def backward_kernel(
    a_ref, h_ref, dy_ref, wg_ref, wu_ref, wd_ref, gg_ref, gu_ref, gd_ref, squares_ref,
    ct, dag, dau, w, acc, outgoing, incoming, gathered, w_sem, sent_sem, got_sem, write_sem,
):
    rep, me = lax.axis_index("rep"), lax.axis_index("dp")
    at = [me // 16, (me // 4) % 4, me % 4]
    step = [16, 4, 1]
    side, partner = [], []
    for kind in range(2):
        for p, s in zip(at, step):
            other = p + 1 - 2 * (p % 2) if kind == 0 else 3 - p
            side.append(((p + 1) // 2) % 2 if kind == 0 else p // 2)
            partner.append(me + (other - p) * s)
    start = []
    for k in range(COLOURS):
        rows = [0]
        for s in range(6):
            rows.append(rows[-1] + side[(k + s) % 6] * (ROWS >> (s + 1)))
        start.append(rows)

    barrier = pltpu.get_barrier_semaphore()
    for other in partner:
        pl.semaphore_signal(barrier, inc=1, device_id=(rep, other), device_id_type=pl.DeviceIdType.MESH)
    pl.semaphore_wait(barrier, 6)

    squares_ref[...] = jnp.zeros_like(squares_ref)
    ct[0] = dy_ref[...]

    def weights(i):
        layer, at = LAYERS - 1 - i // PER, pl.ds(pl.multiple_of((i % PER) * CH, CH), CH)
        slot = i % 2
        return [
            pltpu.make_async_copy(wg_ref.at[layer, :, at], w.at[slot, 0], w_sem.at[slot, 0]),
            pltpu.make_async_copy(wu_ref.at[layer, :, at], w.at[slot, 1], w_sem.at[slot, 1]),
            pltpu.make_async_copy(wd_ref.at[layer, at, :], w.at[slot, 2], w_sem.at[slot, 2]),
        ]

    def rows_of(start, size):
        return pl.ds(pl.multiple_of(start, 16), size)

    def exchange(c, stage, k):
        even = c % 2
        if stage < 6:
            size, link = ROWS >> (stage + 1), (k + stage) % 6
            part = pl.ds(place(stage), size)
            source, target = outgoing.at[k, part], incoming.at[even, k, part]
        else:
            s = 11 - stage
            size, link = ROWS >> (s + 1), (k + s) % 6
            source = target = gathered.at[c % GATHERS, k, rows_of(start[k][s + 1], size)]
        return pltpu.make_async_remote_copy(
            src_ref=source,
            dst_ref=target,
            send_sem=sent_sem.at[stage, k],
            recv_sem=got_sem.at[even, stage, k],
            device_id=(rep, partner[link]),
            device_id_type=pl.DeviceIdType.MESH,
        )

    def writes(c):
        layer, first = LAYERS - 1 - c // PER, (c % PER) * CH
        slot, copies = c % GATHERS, []
        for k in range(COLOURS):
            matrix, half = k // 2, (k % 2) * 256
            for b in range(4):
                source = gathered.at[slot, k, pl.ds(b * 256, 256)]
                if matrix < 2:
                    to = (gg_ref, gu_ref)[matrix].at[layer, pl.ds(half, 256), pl.ds(pl.multiple_of(first + b * 128, 128), 128)]
                else:
                    to = gd_ref.at[layer, pl.ds(pl.multiple_of(first + half, 256), 256), pl.ds(b * 128, 128)]
                copies.append(pltpu.make_async_copy(source, to, write_sem.at[k, b]))
        return copies

    def stage_of(stage, c):
        slot, even, gather = c % ACCS, c % 2, c % GATHERS
        if stage == 13:
            for copy in writes(c):
                copy.wait()
            return
        for k in range(COLOURS):
            if stage > 0:
                exchange(c, stage - 1, k).wait()
            if stage < 6:
                size = ROWS >> (stage + 1)
                mine, theirs = side[(k + stage) % 6] * size, (1 - side[(k + stage) % 6]) * size
                goes = acc[slot, k, rows_of(start[k][stage] + theirs, size)]
                if stage > 0:
                    base = place(stage - 1)
                    goes += incoming[even, k, rows_of(base + theirs, size)].astype(jnp.float32)
                    stays = rows_of(start[k][stage] + mine, size)
                    acc[slot, k, stays] += incoming[even, k, rows_of(base + mine, size)].astype(jnp.float32)
                outgoing[k, pl.ds(place(stage), size)] = goes.astype(jnp.bfloat16)
            elif stage == 6:
                rows = rows_of(start[k][6], 16)
                total = acc[slot, k, rows] + incoming[even, k, pl.ds(place(5), 16)].astype(jnp.float32)
                gathered[gather, k, rows] = total.astype(jnp.bfloat16)
            if stage < 12:
                exchange(c, stage, k).start()
        if stage == 12:
            for copy in writes(c):
                copy.start()
            for k in range(COLOURS):
                g = gathered[gather, k].astype(jnp.float32)
                squares_ref[...] += jnp.sum((g * g).reshape(ROWS // 8, 8, 128), axis=0)

    def tile_of(i, phase):
        turn, slot, a_slot = i // PER, i % 2, i % ACCS
        tokens = pl.ds(phase * TILE, TILE)
        a, by = a_ref[turn, tokens, :], ct[turn, tokens, :]
        gate = dot(a, w[slot, 0], NN)
        up = dot(a, w[slot, 1], NN)
        by_p = dot(by, w[slot, 2], NT).astype(jnp.bfloat16).astype(jnp.float32)
        sigmoid = 1 / (1 + jnp.exp(-gate))
        silu = gate * sigmoid
        p = (silu * up).astype(jnp.bfloat16)
        by_up = (by_p * silu).astype(jnp.bfloat16)
        by_gate = (by_p * up * (sigmoid * (1 + gate * (1 - sigmoid)))).astype(jnp.bfloat16)
        for matrix, (l, r) in enumerate(((a, by_gate), (a, by_up), (p, by))):
            g = dot(l, r, TN)
            for half in range(2):
                for b in range(4):
                    part = g[half * 256 : half * 256 + 256, b * 128 : b * 128 + 128]
                    if phase == 0:
                        acc[a_slot, 2 * matrix + half, pl.ds(b * 256, 256)] = part
                    else:
                        acc[a_slot, 2 * matrix + half, pl.ds(b * 256, 256)] += part

        @pl.when(i < PER)
        def _():
            dag[tokens, :] += dot(by_gate, w[slot, 0], NT)
            dau[tokens, :] += dot(by_up, w[slot, 1], NT)

    def next_layer():
        def body(t, _):
            tokens = pl.ds(pl.multiple_of(t * 256, 256), 256)
            d = (dag[tokens, :].astype(jnp.bfloat16).astype(jnp.float32) + dau[tokens, :].astype(jnp.bfloat16).astype(jnp.float32)).astype(jnp.bfloat16)
            d, wide = d.astype(jnp.float32), h_ref[tokens, :].astype(jnp.float32)
            s = scale_of(wide)
            by = d * s - wide * (s * s * s * jnp.sum(d * wide, -1, keepdims=True) * (1 / D))
            ct[1, tokens, :] = (ct[0, tokens, :].astype(jnp.float32) + by.astype(jnp.bfloat16).astype(jnp.float32)).astype(jnp.bfloat16)
            return 0

        lax.fori_loop(0, T // 256, body, 0)

    def clear(t, _):
        tokens = pl.ds(pl.multiple_of(t * 256, 256), 256)
        dag[tokens, :] = jnp.zeros((256, D), jnp.float32)
        dau[tokens, :] = jnp.zeros((256, D), jnp.float32)
        return 0

    for copy in weights(0):
        copy.start()
    lax.fori_loop(0, T // 256, clear, 0)

    def body(i, _):
        @pl.when(i < N)
        def _():
            for copy in weights(i):
                copy.wait()

        @pl.when(i + 1 < N)
        def _():
            for copy in weights(i + 1):
                copy.start()

        pl.when(i == PER)(next_layer)

        for phase in range(PHASES):
            pl.when(i < N)(functools.partial(tile_of, i, phase))
            for stage in reversed(range(len(AT))):
                if AT[stage] % PHASES == phase:
                    c = i - AT[stage] // PHASES
                    pl.when((c >= 0) & (c < N))(functools.partial(stage_of, stage, c))
        return 0

    lax.fori_loop(0, N + AT[-1] // PHASES, body, 0)


def backward(a, h, dy, wg, wu, wd):
    vmem, anywhere = pl.BlockSpec(memory_space=pltpu.VMEM), pl.BlockSpec(memory_space=pl.ANY)
    dma = pltpu.SemaphoreType.DMA
    return pl.pallas_call(
        backward_kernel,
        in_specs=[vmem] * 3 + [anywhere] * 3,
        out_specs=[anywhere] * 3 + [vmem],
        out_shape=[
            jax.ShapeDtypeStruct((LAYERS, D, FF), jnp.bfloat16),
            jax.ShapeDtypeStruct((LAYERS, D, FF), jnp.bfloat16),
            jax.ShapeDtypeStruct((LAYERS, FF, D), jnp.bfloat16),
            jax.ShapeDtypeStruct((8, 128), jnp.float32),
        ],
        scratch_shapes=[
            pltpu.VMEM((2, T, D), jnp.bfloat16),
            pltpu.VMEM((T, D), jnp.float32),
            pltpu.VMEM((T, D), jnp.float32),
            pltpu.VMEM((2, 3, D, CH), jnp.bfloat16),
            pltpu.VMEM((ACCS, COLOURS, ROWS, 128), jnp.float32),
            pltpu.VMEM((COLOURS, ROWS, 128), jnp.bfloat16),
            pltpu.VMEM((2, COLOURS, ROWS, 128), jnp.bfloat16),
            pltpu.VMEM((GATHERS, COLOURS, ROWS, 128), jnp.bfloat16),
            dma((2, 3)),
            dma((12, COLOURS)),
            dma((2, 12, COLOURS)),
            dma((COLOURS, 4)),
        ],
        compiler_params=pltpu.CompilerParams(collective_id=0, has_side_effects=True, vmem_limit_bytes=VMEM_LIMIT),
    )(a, h, dy, wg, wu, wd)


def adamw(w, m, v, g):
    m = 0.9 * m + 0.1 * g
    v = 0.95 * v + 0.05 * g * g
    step = m * lax.rsqrt(v + 1e-8) + 0.1 * w
    return (w - 0.02 * step).astype(jnp.bfloat16), m, v


def solution(mesh):
    def step(x, dy, *arrays):
        weights, m, v = (arrays[i : i + 3] for i in (0, 3, 6))
        h, a = forward(x[0], *weights)
        *gradients, squares = backward(a, h, dy[0], *weights)
        count = sum(g.size for g in gradients)
        factor = jnp.minimum(1.0, 0.5 * lax.rsqrt(jnp.sum(squares) / count + 1e-30))
        new = [adamw(w.astype(jnp.float32), m, v, g.astype(jnp.float32) * factor) for w, m, v, g in zip(weights, m, v, gradients, strict=True)]
        return tuple(one[which] for which in range(3) for one in new)

    return jax.shard_map(
        step,
        mesh=mesh,
        in_specs=(P(("rep", "dp"), None, None),) * 2 + (P(None, None, None),) * 9,
        out_specs=(P("rep", None, None),) * 9,
        check_vma=False,
    )
```

time: 732 us -> 445 us (0.61); the launches traced: 725 us -> 445 us
  Pallas kernels: 0 us -> 353 us
  matrix products: 318 us -> 0 us
  waiting for transfers between devices: 275 us -> 0 us
  other arithmetic: 108 us -> 90.9 us
  between operations: 16.4 us -> 1.36 us
    pallas_call x0 -> x2, Pallas kernels: none -> 353 us  [the longest x1 313 us: backward(): pl.pallas_call(backward_kernel, in_specs=[vmem] * 3 + [anywhere] * 3, out...]
    dot_general x15 -> x0, matrix products: 318 us -> none  [the longest x5 118 us: layer(): gate = jnp.dot(a, w['w_gate'], preferred_element_type=jnp.float32)]
    psum x1 -> x0, waiting for transfers between devices: 275 us -> none  [step(): summed[number] = [lax.psum(by_w[name], 'dp') for name in NAMES]]
    reduce_sum x4 -> x1, other arithmetic: 20.2 us -> 1.29 us  [step(): factor = jnp.minimum(1.0, 0.5 * lax.rsqrt(jnp.sum(squares) / count + 1e-30))]
  transfers between devices with their start and end apart: 1 -> 0, of which waited for: 1 -> 0; matrix products, arithmetic and copies ran while one was open for 0% -> 0% of each run, Pallas kernels for 0% -> 0%
where the time goes in v1:
time: 445 us
  Pallas kernels  353 us (79%)
  other arithmetic  90.9 us (20%)
    pallas_call x1, Pallas kernels, backward(): pl.pallas_call(backward_kernel, in_specs=[vmem] * 3 + [anywhere] * 3, out...  313 us
    convert_element_type x2, other arithmetic, adamw(): return ((w - 0.02 * step).astype(jnp.bfloat16), m, v)  89.6 us
    pallas_call x1, Pallas kernels, forward(): pl.pallas_call(forward_kernel, grid=(T // tile,), in_specs=[pl.BlockSpec(...  40 us

profile of v1, /device:TPU:0, one launch (start us, length us, event | category | flops | bytes accessed | tf_op | source)
XLA Modules:
  0.0 445.2 jit_solution(9411817727050107203)
XLA Ops:
  0.6 40.0 %shard_map.178 = (bf16[2048,512]{1,0:T(8,128)(2,1)}, bf16[2,2048,512]{2,1,0:T(8,128)(2,1)}) custom-call(bf16[2048,512]{1,0:T(8,128)(2,1)} %bitcast.3, bf16[2,512,4096]{2,1,0:T(8,128)(2,1)} %wg_ref.3, bf16[2,512,4096]{2,1,0:T(8,128)(2,1)} %wu_ref.3, bf16[2,4096,512]{2,1,0:T(8,128)(2,1)} %wd_ref.3), custom_call_target="tpu_custom_call" | custom-call | tf_op jit(solution)/shard_map/pallas_call | solution.py:57
  40.7 312.9 %shard_map.179 = (bf16[2,512,4096]{2,1,0:T(8,128)(2,1)}, bf16[2,512,4096]{2,1,0:T(8,128)(2,1)}, bf16[2,4096,512]{2,1,0:T(8,128)(2,1)}, f32[8,128]{1,0:T(8,128)}) custom-call(bf16[2,2048,512]{2,1,0:T(8,128)(2,1)} %get-tuple-element.15.a_ref, bf16[2048,512]{1,0:T(8,128)(2,1)} %get-tuple-element.16.h_ref, bf16[2048,512]{1,0:T(8,128)(2,1)} %bitcast.2, ...), custom_call_target="tpu_custom_call" | custom-call | tf_op jit(solution)/shard_map/pallas_call | solution.py:252
  353.6 1.3 reduce_sum.9
  355.6 0.0 copy-start
  355.6 61.6 %fusion.2 = (bf16[2,512,4096]{2,1,0:T(8,128)(2,1)}, f32[2,512,4096]{2,1,0:T(8,128)}, f32[2,512,4096]{2,1,0:T(8,128)}, bf16[2,512,4096]{2,1,0:T(8,128)(2,1)}, f32...) fusion(bf16[2,512,4096]{2,1,0:T(8,128)(2,1)} %wg_ref.3, f32[]{:T(128)S(6)} %min_shard_map.3, ...), kind=kLoop, calls=%fused_computation.11 | loop fusion | flops 142606336 | bytes 184549376 | tf_op jit(solution)/shard_map/convert_element_type | solution.py:284
  417.2 0.0 copy-done
  417.2 28.0 %fusion.8 = (bf16[2,4096,512]{2,1,0:T(8,128)(2,1)}, f32[2,4096,512]{2,1,0:T(8,128)}, f32[2,4096,512]{2,1,0:T(8,128)}) fusion(bf16[2,4096,512]{2,1,0:T(8,128)(2,1)} %wd_ref.3, f32[]{:T(128)S(6)} %min_shard_map.3, bf16[2,4096,512]{2,1,0:T(8,128)(2,1)S(1)} %copy-done, f32[2,4096,512]{2,1,0:T(8,128)} %param.21, f32[2,4096,512]{2,1,0:T(8,128)} %param.18), kind=kLoop, calls=%fused_computation.17 | loop fusion | flops 71303168 | bytes 92274688 | tf_op jit(solution)/shard_map/convert_element_type | solution.py:284
Async XLA Ops:
  355.6 61.6 %copy-start = (bf16[2,4096,512]{2,1,0:T(8,128)(2,1)S(1)}, bf16[2,4096,512]{2,1,0:T(8,128)(2,1)}, u32[]{:S(2)}) copy-start(bf16[2,4096,512]{2,1,0:T(8,128)(2,1)} %get-tuple-element.20) | copy-start | bytes 25165828

commit v2 on v1

--- a/solution.py
+++ b/solution.py
@@ -16,8 +16,8 @@
 PHASES = T // TILE
 COLOURS = 6
 ROWS = 1024
-AT = [3 + o for o in (0, 2, 4, 5, 6, 7, 8, 9, 10, 11, 12, 14, 16, 17)]
-ACCS, GATHERS = 3, 4
+AT = [3 + o for o in (0, 4, 7, 9, 11, 13, 15, 17, 19, 21, 23, 26, 30, 31)]
+ACCS, GATHERS = 5, 5
 VMEM_LIMIT = 66_000_000
 
 dot = functools.partial(lax.dot_general, preferred_element_type=jnp.float32)
@@ -35,42 +35,13 @@
     return (wide * scale_of(wide)).astype(jnp.bfloat16)
 
 
-def forward_kernel(x_ref, wg_ref, wu_ref, wd_ref, h_ref, a_ref):
-    x = x_ref[...]
-    a = normed(x)
-    a_ref[1] = a
-    y = jnp.zeros(x.shape, jnp.float32)
-    for c in range(FF // CH):
-        at = pl.ds(c * CH, CH)
-        gate = dot(a, wg_ref[0, :, at], NN)
-        up = dot(a, wu_ref[0, :, at], NN)
-        p = (gate * (1 / (1 + jnp.exp(-gate))) * up).astype(jnp.bfloat16)
-        y += dot(p, wd_ref[0, at, :], NN)
-    h = (x.astype(jnp.float32) + y.astype(jnp.bfloat16).astype(jnp.float32)).astype(jnp.bfloat16)
-    h_ref[...] = h
-    a_ref[0] = normed(h)
-
-
-def forward(x, wg, wu, wd):
-    tile = 256
-    whole = lambda s: pl.BlockSpec(s, lambda i: (0, 0, 0), pipeline_mode=pl.Buffered(1))
-    return pl.pallas_call(
-        forward_kernel,
-        grid=(T // tile,),
-        in_specs=[pl.BlockSpec((tile, D), lambda i: (i, 0)), whole((1, D, FF)), whole((1, D, FF)), whole((1, FF, D))],
-        out_specs=[pl.BlockSpec((tile, D), lambda i: (i, 0)), pl.BlockSpec((2, tile, D), lambda i: (0, i, 0))],
-        out_shape=[jax.ShapeDtypeStruct((T, D), jnp.bfloat16), jax.ShapeDtypeStruct((2, T, D), jnp.bfloat16)],
-        compiler_params=pltpu.CompilerParams(vmem_limit_bytes=VMEM_LIMIT),
-    )(x, wg, wu, wd)
-
-
 def place(stage):
     return ROWS - (ROWS >> stage)
 
 
-def backward_kernel(
-    a_ref, h_ref, dy_ref, wg_ref, wu_ref, wd_ref, gg_ref, gu_ref, gd_ref, squares_ref,
-    ct, dag, dau, w, acc, outgoing, incoming, gathered, w_sem, sent_sem, got_sem, write_sem,
+def kernel(
+    x_ref, dy_ref, wg_ref, wu_ref, wd_ref, gg_ref, gu_ref, gd_ref, squares_ref,
+    h_ref, a_ref, ct, dag, dau, w, acc, outgoing, incoming, gathered, in_sem, w_sem, sent_sem, got_sem, write_sem,
 ):
     rep, me = lax.axis_index("rep"), lax.axis_index("dp")
     at = [me // 16, (me // 4) % 4, me % 4]
@@ -91,14 +62,11 @@
     barrier = pltpu.get_barrier_semaphore()
     for other in partner:
         pl.semaphore_signal(barrier, inc=1, device_id=(rep, other), device_id_type=pl.DeviceIdType.MESH)
-    pl.semaphore_wait(barrier, 6)
-
     squares_ref[...] = jnp.zeros_like(squares_ref)
-    ct[0] = dy_ref[...]
 
     def weights(i):
-        layer, at = LAYERS - 1 - i // PER, pl.ds(pl.multiple_of((i % PER) * CH, CH), CH)
-        slot = i % 2
+        layer, at = ((i + PER) // PER) % 2, pl.ds(pl.multiple_of(((i + PER) % PER) * CH, CH), CH)
+        slot = (i + PER) % 2
         return [
             pltpu.make_async_copy(wg_ref.at[layer, :, at], w.at[slot, 0], w_sem.at[slot, 0]),
             pltpu.make_async_copy(wu_ref.at[layer, :, at], w.at[slot, 1], w_sem.at[slot, 1]),
@@ -212,15 +180,49 @@
 
         lax.fori_loop(0, T // 256, body, 0)
 
-    def clear(t, _):
+    def first(t, _):
         tokens = pl.ds(pl.multiple_of(t * 256, 256), 256)
+        a_ref[1, tokens, :] = normed(h_ref[tokens, :])
+        dag[tokens, :] = jnp.zeros((256, D), jnp.float32)
+        return 0
+
+    def forward(i, _):
+        for copy in weights(i):
+            copy.wait()
+        for copy in weights(i + 1):
+            copy.start()
+        slot = (i + PER) % 2
+
+        def tile(t, _):
+            tokens = pl.ds(pl.multiple_of(t * TILE, TILE), TILE)
+            a = a_ref[1, tokens, :]
+            gate = dot(a, w[slot, 0], NN)
+            up = dot(a, w[slot, 1], NN)
+            p = (gate * (1 / (1 + jnp.exp(-gate))) * up).astype(jnp.bfloat16)
+            dag[tokens, :] += dot(p, w[slot, 2], NN)
+            return 0
+
+        lax.fori_loop(0, PHASES, tile, 0)
+        return 0
+
+    def second(t, _):
+        tokens = pl.ds(pl.multiple_of(t * 256, 256), 256)
+        h = (h_ref[tokens, :].astype(jnp.float32) + dag[tokens, :].astype(jnp.bfloat16).astype(jnp.float32)).astype(jnp.bfloat16)
+        h_ref[tokens, :] = h
+        a_ref[0, tokens, :] = normed(h)
         dag[tokens, :] = jnp.zeros((256, D), jnp.float32)
         dau[tokens, :] = jnp.zeros((256, D), jnp.float32)
         return 0
 
-    for copy in weights(0):
+    inputs = [pltpu.make_async_copy(x_ref, h_ref, in_sem.at[0]), pltpu.make_async_copy(dy_ref, ct.at[0], in_sem.at[1])]
+    for copy in inputs + weights(-PER):
         copy.start()
-    lax.fori_loop(0, T // 256, clear, 0)
+    inputs[0].wait()
+    lax.fori_loop(0, T // 256, first, 0)
+    lax.fori_loop(-PER, 0, forward, 0)
+    lax.fori_loop(0, T // 256, second, 0)
+    inputs[1].wait()
+    pl.semaphore_wait(barrier, 6)
 
     def body(i, _):
         @pl.when(i < N)
@@ -246,12 +248,12 @@
     lax.fori_loop(0, N + AT[-1] // PHASES, body, 0)
 
 
-def backward(a, h, dy, wg, wu, wd):
+def gradients_of(x, dy, wg, wu, wd):
     vmem, anywhere = pl.BlockSpec(memory_space=pltpu.VMEM), pl.BlockSpec(memory_space=pl.ANY)
     dma = pltpu.SemaphoreType.DMA
     return pl.pallas_call(
-        backward_kernel,
-        in_specs=[vmem] * 3 + [anywhere] * 3,
+        kernel,
+        in_specs=[anywhere] * 5,
         out_specs=[anywhere] * 3 + [vmem],
         out_shape=[
             jax.ShapeDtypeStruct((LAYERS, D, FF), jnp.bfloat16),
@@ -260,6 +262,8 @@
             jax.ShapeDtypeStruct((8, 128), jnp.float32),
         ],
         scratch_shapes=[
+            pltpu.VMEM((T, D), jnp.bfloat16),
+            pltpu.VMEM((2, T, D), jnp.bfloat16),
             pltpu.VMEM((2, T, D), jnp.bfloat16),
             pltpu.VMEM((T, D), jnp.float32),
             pltpu.VMEM((T, D), jnp.float32),
@@ -268,13 +272,14 @@
             pltpu.VMEM((COLOURS, ROWS, 128), jnp.bfloat16),
             pltpu.VMEM((2, COLOURS, ROWS, 128), jnp.bfloat16),
             pltpu.VMEM((GATHERS, COLOURS, ROWS, 128), jnp.bfloat16),
+            dma((2,)),
             dma((2, 3)),
             dma((12, COLOURS)),
             dma((2, 12, COLOURS)),
             dma((COLOURS, 4)),
         ],
         compiler_params=pltpu.CompilerParams(collective_id=0, has_side_effects=True, vmem_limit_bytes=VMEM_LIMIT),
-    )(a, h, dy, wg, wu, wd)
+    )(x, dy, wg, wu, wd)
 
 
 def adamw(w, m, v, g):
@@ -287,8 +292,7 @@
 def solution(mesh):
     def step(x, dy, *arrays):
         weights, m, v = (arrays[i : i + 3] for i in (0, 3, 6))
-        h, a = forward(x[0], *weights)
-        *gradients, squares = backward(a, h, dy[0], *weights)
+        *gradients, squares = gradients_of(x[0], dy[0], *weights)
         count = sum(g.size for g in gradients)
         factor = jnp.minimum(1.0, 0.5 * lax.rsqrt(jnp.sum(squares) / count + 1e-30))
         new = [adamw(w.astype(jnp.float32), m, v, g.astype(jnp.float32) * factor) for w, m, v, g in zip(weights, m, v, gradients, strict=True)]

time: 445 us -> 389 us (0.87)
  Pallas kernels: 353 us -> 296 us
    pallas_call x2 -> x1, Pallas kernels: 353 us -> 296 us  [gradients_of(): pl.pallas_call(kernel, in_specs=[anywhere] * 5, out_specs=[anywhere] * 3...]
where the time goes in v2:
time: 389 us
  Pallas kernels  296 us (76%)
  other arithmetic  91 us (23%)
    pallas_call x1, Pallas kernels, gradients_of(): pl.pallas_call(kernel, in_specs=[anywhere] * 5, out_specs=[anywhere] * 3...  296 us
    convert_element_type x2, other arithmetic, adamw(): return ((w - 0.02 * step).astype(jnp.bfloat16), m, v)  89.7 us

profile of v2, /device:TPU:0, one launch (start us, length us, event | category | flops | bytes accessed | tf_op | source)
XLA Modules:
  0.0 388.8 jit_solution(5456160401135508585)
XLA Ops:
  0.6 296.4 %shard_map.178 = (bf16[2,512,4096]{2,1,0:T(8,128)(2,1)}, bf16[2,512,4096]{2,1,0:T(8,128)(2,1)}, bf16[2,4096,512]{2,1,0:T(8,128)(2,1)}, f32[8,128]{1,0:T(8,128)}) custom-call(bf16[2048,512]{1,0:T(8,128)(2,1)} %bitcast.2, bf16[2048,512]{1,0:T(8,128)(2,1)} %bitcast.3, bf16[2,512,4096]{2,1,0:T(8,128)(2,1)} %wg_ref.1, bf16[2,512,4096]{2,1,0:T(8,128)(2,1)} %wu_ref.1, ...), custom_call_target="tpu_custom_call" | custom-call | tf_op jit(solution)/shard_map/pallas_call | solution.py:254
  297.1 1.3 reduce_sum.9
  299.0 0.0 copy-start
  299.0 61.6 %fusion.2 = (bf16[2,512,4096]{2,1,0:T(8,128)(2,1)}, f32[2,512,4096]{2,1,0:T(8,128)}, f32[2,512,4096]{2,1,0:T(8,128)}, bf16[2,512,4096]{2,1,0:T(8,128)(2,1)}, f32...) fusion(bf16[2,512,4096]{2,1,0:T(8,128)(2,1)} %wg_ref.1, f32[]{:T(128)S(6)} %min_shard_map.3, ...), kind=kLoop, calls=%fused_computation.11 | loop fusion | flops 142606336 | bytes 184549376 | tf_op jit(solution)/shard_map/convert_element_type | solution.py:289
  360.6 0.0 copy-done
  360.6 28.1 %fusion.8 = (bf16[2,4096,512]{2,1,0:T(8,128)(2,1)}, f32[2,4096,512]{2,1,0:T(8,128)}, f32[2,4096,512]{2,1,0:T(8,128)}) fusion(bf16[2,4096,512]{2,1,0:T(8,128)(2,1)S(1)} %copy-done, f32[]{:T(128)S(6)} %min_shard_map.3, bf16[2,4096,512]{2,1,0:T(8,128)(2,1)} %get-tuple-element.16, f32[2,4096,512]{2,1,0:T(8,128)} %param.21, f32[2,4096,512]{2,1,0:T(8,128)} %param.18), kind=kLoop, calls=%fused_computation.17 | loop fusion | flops 71303168 | bytes 92274688 | tf_op jit(solution)/shard_map/convert_element_type | solution.py:289
Async XLA Ops:
  299.0 61.6 %copy-start = (bf16[2,4096,512]{2,1,0:T(8,128)(2,1)S(1)}, bf16[2,4096,512]{2,1,0:T(8,128)(2,1)}, u32[]{:S(2)}) copy-start(bf16[2,4096,512]{2,1,0:T(8,128)(2,1)} %wd_ref.1) | copy-start | bytes 25165828

commit v3 on v2

--- a/solution.py
+++ b/solution.py
@@ -16,8 +16,8 @@
 PHASES = T // TILE
 COLOURS = 6
 ROWS = 1024
-AT = [3 + o for o in (0, 4, 7, 9, 11, 13, 15, 17, 19, 21, 23, 26, 30, 31)]
-ACCS, GATHERS = 5, 5
+AT = [3 + o for o in (0, 4, 8, 11, 14, 16, 18, 20, 22, 24, 27, 31, 35, 36)]
+ACCS, GATHERS = 6, 6
 VMEM_LIMIT = 66_000_000
 
 dot = functools.partial(lax.dot_general, preferred_element_type=jnp.float32)

time: 389 us -> 396 us (1.018)
  Pallas kernels: 296 us -> 304 us
    pallas_call x1, Pallas kernels: 296 us -> 304 us  [gradients_of(): pl.pallas_call(kernel, in_specs=[anywhere] * 5, out_specs=[anywhere] * 3...]
where the time goes in v3:
time: 396 us
  Pallas kernels  304 us (77%)
  other arithmetic  91 us (23%)
    pallas_call x1, Pallas kernels, gradients_of(): pl.pallas_call(kernel, in_specs=[anywhere] * 5, out_specs=[anywhere] * 3...  304 us
    convert_element_type x2, other arithmetic, adamw(): return ((w - 0.02 * step).astype(jnp.bfloat16), m, v)  89.7 us

profile of v3, /device:TPU:0, one launch (start us, length us, event | category | flops | bytes accessed | tf_op | source)
XLA Modules:
  0.0 396.2 jit_solution(5068329617012879466)
XLA Ops:
  0.6 303.9 %shard_map.178 = (bf16[2,512,4096]{2,1,0:T(8,128)(2,1)}, bf16[2,512,4096]{2,1,0:T(8,128)(2,1)}, bf16[2,4096,512]{2,1,0:T(8,128)(2,1)}, f32[8,128]{1,0:T(8,128)}) custom-call(bf16[2048,512]{1,0:T(8,128)(2,1)} %bitcast.2, bf16[2048,512]{1,0:T(8,128)(2,1)} %bitcast.3, bf16[2,512,4096]{2,1,0:T(8,128)(2,1)} %wg_ref.1, bf16[2,512,4096]{2,1,0:T(8,128)(2,1)} %wu_ref.1, ...), custom_call_target="tpu_custom_call" | custom-call | tf_op jit(solution)/shard_map/pallas_call | solution.py:254
  304.6 1.3 reduce_sum.9
  306.5 0.0 copy-start
  306.5 61.6 %fusion.2 = (bf16[2,512,4096]{2,1,0:T(8,128)(2,1)}, f32[2,512,4096]{2,1,0:T(8,128)}, f32[2,512,4096]{2,1,0:T(8,128)}, bf16[2,512,4096]{2,1,0:T(8,128)(2,1)}, f32...) fusion(bf16[2,512,4096]{2,1,0:T(8,128)(2,1)} %wg_ref.1, f32[]{:T(128)S(6)} %min_shard_map.3, ...), kind=kLoop, calls=%fused_computation.11 | loop fusion | flops 142606336 | bytes 184549376 | tf_op jit(solution)/shard_map/convert_element_type | solution.py:289
  368.1 0.0 copy-done
  368.1 28.1 %fusion.8 = (bf16[2,4096,512]{2,1,0:T(8,128)(2,1)}, f32[2,4096,512]{2,1,0:T(8,128)}, f32[2,4096,512]{2,1,0:T(8,128)}) fusion(bf16[2,4096,512]{2,1,0:T(8,128)(2,1)S(1)} %copy-done, f32[]{:T(128)S(6)} %min_shard_map.3, bf16[2,4096,512]{2,1,0:T(8,128)(2,1)} %get-tuple-element.16, f32[2,4096,512]{2,1,0:T(8,128)} %param.21, f32[2,4096,512]{2,1,0:T(8,128)} %param.18), kind=kLoop, calls=%fused_computation.17 | loop fusion | flops 71303168 | bytes 92274688 | tf_op jit(solution)/shard_map/convert_element_type | solution.py:289
Async XLA Ops:
  306.5 61.6 %copy-start = (bf16[2,4096,512]{2,1,0:T(8,128)(2,1)S(1)}, bf16[2,4096,512]{2,1,0:T(8,128)(2,1)}, u32[]{:S(2)}) copy-start(bf16[2,4096,512]{2,1,0:T(8,128)(2,1)} %wd_ref.1) | copy-start | bytes 25165828
